TPU v7x, 32 devices: a 4x2x2 block of a 4x4x8 slice. The times are simulated.
32 devices in a mesh: dp: 4 (over y, z), sp: 8 (over x, core).
Axes of the slice: x: 4, y: 2, z: 2, core: 2. Of those that a mesh axis runs over, the one named last changes fastest.
The devices are a block of a 4x4x8 slice.
Arguments:
- hidden: bfloat16 [4096, 2048], P(('dp', 'sp')), parts along dimension 0
- positions: int32 [4096], P(('dp', 'sp')), parts along dimension 0
- d_attn: bfloat16 [4096, 2048], P(('dp', 'sp')), parts along dimension 0
- ln_weight: bfloat16 [2048], replicated
- w_q: bfloat16 [2048, 2048], replicated
- w_k: bfloat16 [2048, 2048], replicated
- w_v: bfloat16 [2048, 2048], replicated
- w_o: bfloat16 [2048, 2048], replicated
Outputs:
- output 1: bfloat16 [4096, 2048], P(('dp', 'sp')), parts along dimension 0
- output 2: bfloat16 [4096, 2048], P(('dp', 'sp')), parts along dimension 0
- output 3: bfloat16 [8192], P('dp'), parts along dimension 0
- output 4: bfloat16 [8192, 2048], P('dp'), parts along dimension 0
- output 5: bfloat16 [8192, 2048], P('dp'), parts along dimension 0
- output 6: bfloat16 [8192, 2048], P('dp'), parts along dimension 0
- output 7: bfloat16 [8192, 2048], P('dp'), parts along dimension 0
There are 4 independent parts. A program takes and returns all parts, laid end to end along the dimension named above; an argument that names none is the same for every part.
All inputs are finite; a program needn't handle non-finite values.
Results may differ from a plain program's by a relative error of at most 0.0120283.
Values are sent between devices in bfloat16 or wider.
A program may use at most 768 MiB of HBM per device.

v0:
```python
import functools

import jax
import jax.numpy as jnp
from jax import lax
from jax.experimental import pallas as pl
from jax.experimental.pallas import tpu as pltpu
from jax.sharding import PartitionSpec as P

HEAD_DIM = 128
LN_EPS = 1e-5
ROPE_BASE = 10000.0
SCALE = HEAD_DIM ** -0.5
LOG2E = 1.4426950408889634
CORES = 2
QB = 256
MT = 256
VMEM_LIMIT = 67043328
MESH = pl.DeviceIdType.MESH
F32 = jnp.float32
BF16 = jnp.bfloat16


def normalize(x):
    x = x.astype(F32)
    centered = x - jnp.mean(x, axis=-1, keepdims=True)
    rstd = lax.rsqrt(jnp.mean(centered * centered, axis=-1, keepdims=True) + LN_EPS)
    return centered * rstd, rstd


def sin_cos(a):
    n = jnp.floor(a * 0.6366197723675814 + 0.5)
    r = ((a - n * 1.5703125) - n * 4.8375129699707031e-4) - n * 7.5497899548918821e-8
    z = r * r
    s = r + r * z * (-1.6666654611e-1 + z * (8.3321608736e-3 + z * -1.9515295891e-4))
    c = 1.0 - 0.5 * z + z * z * (4.166664568298827e-2 + z * (-1.388731625493765e-3 + z * 2.443315711809948e-5))
    quad = n.astype(jnp.int32)
    odd = (quad & 1) == 1
    sin = jnp.where(odd, c, s)
    cos = jnp.where(odd, s, c)
    return jnp.where((quad & 2) == 2, -sin, sin), jnp.where(((quad + 1) & 2) == 2, -cos, cos)


def even_lanes(shape):
    return lax.broadcasted_iota(jnp.int32, shape, 1) % 2 == 0


def swap_pairs(y):
    return jnp.where(even_lanes(y.shape), pltpu.roll(y, HEAD_DIM - 1, 1), pltpu.roll(y, 1, 1))


def nt(a, b):
    return lax.dot_general(a, b, (((1,), (1,)), ((), ())), preferred_element_type=F32)


def nn(a, b):
    return jnp.dot(a, b, preferred_element_type=F32)


def main_kernel(n_dev, x_ref, g_ref, p_ref, f_ref, w_ref, wq, wk, wv, wo,
                h_out, g_out, o_out, gq_out, gk_out, gv_out, a_out, dx_out, dl_out,
                h_all, g_all, pos, cos_s, sin_s, w3, wo_s, qkv, do_s,
                res, m_s, li_s, kt_s, vt_s, pt_s, dst_s, a_part, a_recv, dh_part, dh_recv, dl_buf,
                ssem, rsem, wsem, lsem, xsem, osem, psem, dsem, fsem):
    blk, model = x_ref.shape
    half = blk // 2
    rows_chip = CORES * blk
    n_chips = n_dev // CORES
    heads = qkv.shape[1]
    width = heads * HEAD_DIM
    seq = n_dev * blk
    nq = seq // QB

    me = lax.axis_index("sp")
    chip, core = me // CORES, lax.rem(me, CORES)
    other = 1 - core

    def dev(step, cr):
        return lax.rem(chip + step + n_chips, n_chips) * CORES + cr

    partner, right, left = dev(0, other), dev(1, core), dev(-1, core)
    others = [lax.rem(me + k, n_dev) for k in range(1, n_dev)]

    barrier = pltpu.get_barrier_semaphore()
    for d in others:
        pl.semaphore_signal(barrier, inc=1, device_id={"sp": d}, device_id_type=MESH)

    col0 = pl.multiple_of(core * width, width)
    wcopies = [
        pltpu.make_async_copy(w.at[:, pl.ds(col0, width)], w3.at[j], wsem.at[j])
        for j, w in enumerate((wq, wk, wv))
    ]
    wcopies.append(pltpu.make_async_copy(wo.at[pl.ds(col0, width), :], wo_s, wsem.at[3]))
    for c in wcopies:
        c.start()

    own = pl.ds(pl.multiple_of(me * blk, blk), blk)
    ln_w = w_ref[...].astype(F32).reshape(1, model)
    h_all[own, :] = (normalize(x_ref[...])[0] * ln_w).astype(BF16)
    g_all[own, :] = g_ref[...]
    pos[me] = p_ref[...].reshape(1, blk)

    arrays = (h_all, g_all)

    def region(block, piece):
        if piece is None:
            return pl.ds(pl.multiple_of(block * blk, blk), blk)
        return pl.ds(pl.multiple_of(block * blk + piece * half, half), half)

    def copy(a, kind, block, piece, to):
        r = region(block, piece)
        return pltpu.make_async_remote_copy(
            src_ref=arrays[a].at[r, :], dst_ref=arrays[a].at[r, :],
            send_sem=ssem.at[a, kind], recv_sem=rsem.at[a, kind],
            device_id={"sp": to}, device_id_type=MESH)

    far = 2
    sends = {
        0: (me, None, partner),
        1: (me, 0, right), 2: (me, 1, right),
        3: (me, 0, left), 4: (me, 1, left),
        5: (dev(-1, core), 0, right), 6: (dev(1, core), 1, left),
        7: (dev(-1, core), 0, partner), 8: (dev(-1, core), 1, partner),
        9: (dev(1, core), 0, partner), 10: (dev(1, core), 1, partner),
        11: (dev(far, core), 0, partner), 12: (dev(far, core), 1, partner),
    }
    recvs = {
        0: (partner, None),
        1: (dev(-1, core), 0), 2: (dev(-1, core), 1),
        3: (dev(1, core), 0), 4: (dev(1, core), 1),
        5: (dev(far, core), 0), 6: (dev(far, core), 1),
        7: (dev(-1, other), 0), 8: (dev(-1, other), 1),
        9: (dev(1, other), 0), 10: (dev(1, other), 1),
        11: (dev(far, other), 0), 12: (dev(far, other), 1),
    }

    def send(a, kind):
        block, piece, to = sends[kind]
        copy(a, kind, block, piece, to).start()

    def got(a, kind):
        block, piece = recvs[kind]
        copy(a, kind, block, piece, partner).wait_recv()

    def small(buf, sems, k, source, to):
        return pltpu.make_async_remote_copy(
            src_ref=buf.at[source], dst_ref=buf.at[source],
            send_sem=sems.at[0, k], recv_sem=sems.at[1, k],
            device_id={"sp": to}, device_id_type=MESH)

    def small_send(buf, sems):
        for k in range(1, n_dev):
            small(buf, sems, k, me, others[k - 1]).start()

    def small_wait(buf, sems):
        for k in range(1, n_dev):
            small(buf, sems, k, lax.rem(me - k + n_dev, n_dev), partner).wait_recv()
        for k in range(1, n_dev):
            small(buf, sems, k, me, partner).wait_send()

    pl.semaphore_wait(barrier, n_dev - 1)
    for kind in (1, 4, 2, 3, 0):
        send(0, kind)
    small_send(pos, psem)
    send(1, 0)

    def pass_first(a):
        got(a, 1)
        send(a, 5)
        send(a, 7)
        got(a, 4)
        send(a, 6)
        send(a, 10)

    def pass_second(a):
        got(a, 2)
        send(a, 8)
        got(a, 3)
        send(a, 9)

    def pass_far(a):
        got(a, 5)
        send(a, 11)
        got(a, 6)
        send(a, 12)

    def from_partner(a, which):
        for kind in which:
            got(a, kind)

    def chip_rows(i):
        step = lax.rem(i * (i + 1) // 2, n_chips)
        return pl.ds(pl.multiple_of(lax.rem(chip + step, n_chips) * rows_chip, rows_chip), rows_chip)

    def fill_tables():
        small_wait(pos, psem)
        diag = (lax.broadcasted_iota(jnp.int32, (blk, blk), 0)
                == lax.broadcasted_iota(jnp.int32, (blk, blk), 1))
        even = even_lanes((blk, HEAD_DIM))

        @pl.loop(0, n_dev)
        def _(b):
            r = pl.ds(pl.multiple_of(b * blk, blk), blk)
            p = jnp.broadcast_to(pos[b].astype(F32), (blk, blk))
            col = jnp.sum(jnp.where(diag, p, 0.0), axis=1, keepdims=True)
            sin, cos = sin_cos(col * f_ref[...])
            cos_s[r, :] = cos
            sin_s[r, :] = jnp.where(even, -sin, sin)

    @pl.loop(0, 3 * n_chips)
    def _(it):
        i, j = it // 3, lax.rem(it, 3)

        @pl.when(it == 0)
        def _():
            fill_tables()
            got(0, 0)
            for c in wcopies:
                c.wait()

        @pl.when(it == 3)
        def _():
            pass_first(0)
            for kind in (1, 4, 2, 3):
                send(1, kind)
            pass_second(0)
            from_partner(0, (7, 8, 9, 10))

        @pl.when(it == 9)
        def _():
            pass_far(0)
            from_partner(0, (11, 12))

        r = chip_rows(i)
        y = nn(h_all[r, :], w3[j])
        is_v = j == 2
        c = jnp.where(is_v, 1.0, cos_s[r, :])
        s = jnp.where(is_v, 0.0, sin_s[r, :])
        for n in range(heads):
            yn = y[:, n * HEAD_DIM:(n + 1) * HEAD_DIM]
            qkv[j, n, r, :] = (yn * c + swap_pairs(yn) * s).astype(BF16)

    h_copy = pltpu.make_async_copy(h_all, h_out, lsem.at[0])
    h_copy.start()

    outs = (o_out, gq_out, gk_out, gv_out)

    def send_head(a, n):
        cols = pl.ds(pl.multiple_of(core * width + n * HEAD_DIM, HEAD_DIM), HEAD_DIM)
        pltpu.make_async_copy(res.at[a, n], outs[a].at[:, cols], osem.at[a]).start()
        pltpu.make_async_remote_copy(
            src_ref=res.at[a, n], dst_ref=outs[a].at[:, cols],
            send_sem=xsem.at[0, a], recv_sem=xsem.at[1, a],
            device_id={"sp": partner}, device_id_type=MESH).start()

    c2 = SCALE * LOG2E
    causal = (lax.broadcasted_iota(jnp.int32, (QB, QB), 0)
              <= lax.broadcasted_iota(jnp.int32, (QB, QB), 1))

    def tile(i):
        return slice(i * QB, (i + 1) * QB)

    def scores(n, i, j):
        s = nt(qkv[1, n, tile(j), :], qkv[0, n, tile(i), :])
        return jnp.where(causal, s, -jnp.inf) if i == j else s

    @pl.loop(0, heads)
    def _(n):
        @pl.when(n == 2)
        def _():
            got(1, 0)
            pass_first(1)

        vt_s[...] = qkv[2, n].T
        for i in range(nq):
            ss = [scores(n, i, j) for j in range(i + 1)]
            m = functools.reduce(jnp.maximum, [jnp.max(s, axis=0, keepdims=True) for s in ss])
            es = [jnp.exp2((s - m) * c2) for s in ss]
            li = 1.0 / sum(jnp.sum(e, axis=0, keepdims=True) for e in es)
            m_s[n, :, tile(i)] = m
            li_s[n, :, tile(i)] = li
            o_t = sum(nn(vt_s[:, tile(j)], (e * li).astype(BF16)) for j, e in enumerate(es))
            res[0, n, tile(i), :] = o_t.T.astype(BF16)
        send_head(0, n)

    @pl.loop(0, n_chips)
    def _(i):
        @pl.when(i == 1)
        def _():
            pass_second(1)
            from_partner(1, (7, 8, 9, 10))

        @pl.when(i == 3)
        def _():
            pass_far(1)
            from_partner(1, (11, 12))

        r = chip_rows(i)
        y = nt(g_all[r, :], wo_s[...])
        for n in range(heads):
            do_s[n, r, :] = y[:, n * HEAD_DIM:(n + 1) * HEAD_DIM].astype(BF16)

    g_copy = pltpu.make_async_copy(g_all, g_out, lsem.at[1])
    g_copy.start()

    def rows_of(a, r):
        return jnp.concatenate([res[a, n, r, :] for n in range(heads)], axis=1)

    here = pl.ds(pl.multiple_of(chip * rows_chip, rows_chip), rows_chip)
    mine = pl.ds(pl.multiple_of(core * blk, blk), blk)
    theirs = pl.ds(pl.multiple_of(other * blk, blk), blk)

    def swap_part(part, recv, k):
        return pltpu.make_async_remote_copy(
            src_ref=part.at[theirs, :], dst_ref=recv,
            send_sem=fsem.at[0, k], recv_sem=fsem.at[1, k],
            device_id={"sp": partner}, device_id_type=MESH)

    a_part[...] = nn(rows_of(0, here), wo_s[...])
    a_swap = swap_part(a_part, a_recv, 0)
    a_swap.start()

    @pl.loop(0, heads)
    def _(n):
        kt_s[...] = qkv[1, n].T
        for i in range(nq):
            q_i, do_i = qkv[0, n, tile(i), :], do_s[n, tile(i), :]
            m, li = m_s[n, :, tile(i)], li_s[n, :, tile(i)]
            ps, dps = [], []
            rdot = 0.0
            for j in range(i + 1):
                p = jnp.exp2((scores(n, i, j) - m) * c2) * li
                dp = nt(qkv[2, n, tile(j), :], do_i)
                rdot = rdot + jnp.sum(p * dp, axis=0, keepdims=True)
                pt_s[tile(j), tile(i)] = p.astype(BF16)
                ps.append(p)
                dps.append(dp)
            for j in range(i + 1):
                dst_s[tile(j), tile(i)] = (ps[j] * (dps[j] - rdot) * SCALE).astype(BF16)
            dq = nn(kt_s[:, :(i + 1) * QB], dst_s[:(i + 1) * QB, tile(i)]).T.astype(BF16).astype(F32)
            res[1, n, tile(i), :] = (dq * cos_s[tile(i), :] - swap_pairs(dq) * sin_s[tile(i), :]).astype(BF16)
        for j in range(nq):
            dk = nn(dst_s[tile(j), j * QB:], qkv[0, n, j * QB:, :]).astype(BF16).astype(F32)
            res[2, n, tile(j), :] = (dk * cos_s[tile(j), :] - swap_pairs(dk) * sin_s[tile(j), :]).astype(BF16)
            res[3, n, tile(j), :] = nn(pt_s[tile(j), j * QB:], do_s[n, j * QB:, :]).astype(BF16)
        for a in (1, 2, 3):
            send_head(a, n)

    dh_part[...] = sum(nt(rows_of(j + 1, here), w3[j]) for j in range(3))
    dh_swap = swap_part(dh_part, dh_recv, 1)
    dh_swap.start()
    a_swap.wait()
    a_out[...] = (a_part[mine, :] + a_recv[...]).astype(BF16)
    xhat, rstd = normalize(x_ref[...])
    dh_swap.wait()
    dh = dh_part[mine, :] + dh_recv[...]
    dl_buf[me] = jnp.sum(dh * xhat, axis=0, keepdims=True)
    small_send(dl_buf, dsem)
    dy = dh * ln_w
    dx = dy - jnp.mean(dy, axis=-1, keepdims=True) - xhat * jnp.mean(dy * xhat, axis=-1, keepdims=True)
    dx_out[...] = (dx * rstd).astype(BF16)

    h_copy.wait()
    g_copy.wait()
    for a in range(2):
        for kind, (block, piece, to) in sends.items():
            copy(a, kind, block, piece, to).wait_send()
    my_cols = pl.ds(pl.multiple_of(core * width, width), width)
    their_cols = pl.ds(pl.multiple_of(other * width, width), width)
    for a in range(4):
        pltpu.make_async_copy(outs[a].at[:, my_cols], outs[a].at[:, my_cols], osem.at[a]).wait()
        done = pltpu.make_async_remote_copy(
            src_ref=outs[a].at[:, my_cols], dst_ref=outs[a].at[:, their_cols],
            send_sem=xsem.at[0, a], recv_sem=xsem.at[1, a],
            device_id={"sp": partner}, device_id_type=MESH)
        done.wait_send()
        done.wait_recv()
    small_wait(dl_buf, dsem)
    total = dl_buf[0]
    for k in range(1, n_dev):
        total = total + dl_buf[k]
    dl_out[...] = total.astype(BF16).reshape(model)


def run_main(n_dev, hidden, d_attn, positions, ln_weight, w_q, w_k, w_v, w_o):
    blk, model = hidden.shape
    seq = n_dev * blk
    width = w_q.shape[1] // CORES
    heads = width // HEAD_DIM
    vm = pl.BlockSpec(memory_space=pltpu.VMEM)
    hbm = pl.BlockSpec(memory_space=pl.ANY)
    full = jax.ShapeDtypeStruct((seq, model), BF16)
    wide = jax.ShapeDtypeStruct((seq, w_q.shape[1]), BF16)
    rows = jax.ShapeDtypeStruct((blk, model), BF16)
    freq = jnp.repeat(ROPE_BASE ** (-jnp.arange(0, HEAD_DIM, 2, dtype=F32) / HEAD_DIM), 2)[None, :]
    return pl.pallas_call(
        functools.partial(main_kernel, n_dev),
        out_shape=(full, full, wide, wide, wide, wide, rows, rows, jax.ShapeDtypeStruct((model,), BF16)),
        in_specs=[vm] * 5 + [hbm] * 4,
        out_specs=[hbm] * 6 + [vm] * 3,
        scratch_shapes=[
            pltpu.VMEM((seq, model), BF16),
            pltpu.VMEM((seq, model), BF16),
            pltpu.VMEM((n_dev, 1, blk), jnp.int32),
            pltpu.VMEM((seq, HEAD_DIM), F32),
            pltpu.VMEM((seq, HEAD_DIM), F32),
            pltpu.VMEM((3, model, width), BF16),
            pltpu.VMEM((width, model), BF16),
            pltpu.VMEM((3, heads, seq, HEAD_DIM), BF16),
            pltpu.VMEM((heads, seq, HEAD_DIM), BF16),
            pltpu.VMEM((4, heads, seq, HEAD_DIM), BF16),
            pltpu.VMEM((heads, 1, seq), F32),
            pltpu.VMEM((heads, 1, seq), F32),
            pltpu.VMEM((HEAD_DIM, seq), BF16),
            pltpu.VMEM((HEAD_DIM, seq), BF16),
            pltpu.VMEM((seq, seq), BF16),
            pltpu.VMEM((seq, seq), BF16),
            pltpu.VMEM((CORES * blk, model), F32),
            pltpu.VMEM((blk, model), F32),
            pltpu.VMEM((CORES * blk, model), F32),
            pltpu.VMEM((blk, model), F32),
            pltpu.VMEM((n_dev, 1, model), F32),
            pltpu.SemaphoreType.DMA((2, 13)),
            pltpu.SemaphoreType.DMA((2, 13)),
            pltpu.SemaphoreType.DMA((4,)),
            pltpu.SemaphoreType.DMA((2,)),
            pltpu.SemaphoreType.DMA((2, 4)),
            pltpu.SemaphoreType.DMA((4,)),
            pltpu.SemaphoreType.DMA((2, n_dev)),
            pltpu.SemaphoreType.DMA((2, n_dev)),
            pltpu.SemaphoreType.DMA((2, 2)),
        ],
        compiler_params=pltpu.CompilerParams(
            collective_id=0, has_side_effects=True, vmem_limit_bytes=VMEM_LIMIT),
        name="gather_attention",
    )(hidden, d_attn, positions, freq, ln_weight, w_q, w_k, w_v, w_o)


def grad_kernel(h_ref, o_ref, gq, gk, gv, g, dq_ref, dk_ref, dv_ref, do_ref, rhs, sem):
    w, m = pl.program_id(0), pl.program_id(1)

    def load(k):
        src = (gq, gk, gv, g)[k]
        return pltpu.make_async_copy(src, rhs.at[k % 2], sem.at[k % 2])

    for k in range(4):
        @pl.when((w == k) & (m == 0))
        def _():
            if k == 0:
                load(0).start()
            load(k).wait()
            if k < 3:
                load(k + 1).start()

    def tn(a):
        b = rhs[lax.rem(w, 2)]
        return lax.dot_general(a, b, (((0,), (0,)), ((), ())), preferred_element_type=F32).astype(BF16)

    for k, out in enumerate((dq_ref, dk_ref, dv_ref, do_ref)):
        @pl.when(w == k)
        def _():
            out[...] = tn(o_ref[...] if k == 3 else h_ref[...])


def run_grads(h, o, gq, gk, gv, g):
    seq, model = h.shape
    wide = gq.shape[1]
    steps = model // MT
    hbm = pl.BlockSpec(memory_space=pl.ANY)

    def out_spec(k):
        return pl.BlockSpec((MT, wide), lambda w, m: (jnp.where(w == k, m, jnp.where(w < k, 0, steps - 1)), 0))

    return pl.pallas_call(
        grad_kernel,
        grid=(4, steps),
        out_shape=[jax.ShapeDtypeStruct((model, wide), BF16)] * 4,
        in_specs=[
            pl.BlockSpec((seq, MT), lambda w, m: (0, jnp.where(w < 3, m, steps - 1))),
            pl.BlockSpec((seq, MT), lambda w, m: (0, jnp.where(w < 3, 0, m))),
            hbm, hbm, hbm, hbm],
        out_specs=[out_spec(k) for k in range(4)],
        scratch_shapes=[pltpu.VMEM((2, seq, wide), BF16), pltpu.SemaphoreType.DMA((2,))],
        compiler_params=pltpu.CompilerParams(
            dimension_semantics=("arbitrary", "arbitrary"), vmem_limit_bytes=VMEM_LIMIT),
        name="weight_grads",
    )(h, o, gq, gk, gv, g)


def solution(mesh):
    n_dev = mesh.shape['sp']
    row_spec = P(('dp', 'sp'), None)
    full_spec = P(None, None)
    grad_spec = P('dp', None)

    def local_step(hidden, positions, d_attn, ln_weight, w_q, w_k, w_v, w_o):
        h, g, o, gq, gk, gv, attn_out, d_hid, d_lnw = run_main(
            n_dev, hidden, d_attn, positions, ln_weight, w_q, w_k, w_v, w_o)
        return (attn_out, d_hid, d_lnw, *run_grads(h, o, gq, gk, gv, g))

    return jax.shard_map(local_step, mesh=mesh,
                         in_specs=(row_spec, P(('dp', 'sp')), row_spec, P(None), full_spec, full_spec, full_spec, full_spec),
                         out_specs=(row_spec, row_spec, P('dp'), grad_spec, grad_spec, grad_spec, grad_spec),
                         check_vma=False)
```

profile of v0, /device:TPU:81, one launch (start us, length us, event | category | flops | bytes accessed | tf_op | source)
XLA Modules:
  0.0 163.2 jit_solution(15247851963192319289)
XLA Ops:
  0.6 0.1 broadcast_in_dim.3
  0.7 0.7 broadcast_in_dim_reshape.3.f_ref
  1.4 105.5 %gather_attention.1 = (bf16[1024,2048]{1,0:T(8,128)(2,1)}, bf16[1024,2048]{1,0:T(8,128)(2,1)}, bf16[1024,2048]{1,0:T(8,128)(2,1)}, bf16[1024,2048]{1,0:T(8,128)(...) custom-call(bf16[128,2048]{1,0:T(8,128)(2,1)} %x_ref.1, ...), custom_call_target="tpu_custom_call" | custom-call | tf_op jit(solution)/shard_map/gather_attention/pallas_call | solution.py:396
  106.9 51.3 %weight_grads.1 = (bf16[2048,2048]{1,0:T(8,128)(2,1)}, bf16[2048,2048]{1,0:T(8,128)(2,1)}, bf16[2048,2048]{1,0:T(8,128)(2,1)}, bf16[2048,2048]{1,0:T(8,128)(2,1)}) custom-call(bf16[1024,2048]{1,0:T(8,128)(2,1)} %get-tuple-element.23.h_ref, bf16[1024,2048]{1,0:T(8,128)(2,1)} %get-tuple-element.24.o_ref, bf16[1024,2048]{1,0:T(8,128)(2,1)} %get-tuple-element.25.gq, ...), custom_call_target="tpu_custom_call" | custom-call | tf_op jit(solution)/shard_map/weight_grads/pallas_call | solution.py:474
  158.2 1.9 %copy.18 = bf16[128,2048]{1,0:T(8,128)(2,1)} copy(bf16[128,2048]{1,0:T(8,128)(2,1)} %get-tuple-element.40) | data formatting | bytes 1048576
  160.1 1.9 %copy.19 = bf16[128,2048]{1,0:T(8,128)(2,1)} copy(bf16[128,2048]{1,0:T(8,128)(2,1)} %get-tuple-element.41) | data formatting | bytes 1048576
  162.0 1.3 copy.20
  (1 shorter events, 0.0 us)
where the time goes:
time: 164 us; the launch traced here: 163 us
  Pallas kernels  157 us (96%)
  local copies, waits for them, and re-layouts  5.77 us (4%)
    pallas_call x1, Pallas kernels, run_main(): pl.pallas_call(functools.partial(main_kernel, n_dev), out_shape=(full, fu...  105 us
    pallas_call x1, Pallas kernels, run_grads(): pl.pallas_call(grad_kernel, grid=(4, steps), out_shape=[jax.ShapeDtypeStr...  51.3 us
    unnamed x3, local copies, waits for them, and re-layouts  5.03 us

commit v1 on v0

--- a/solution.py
+++ b/solution.py
@@ -14,7 +14,8 @@
 LOG2E = 1.4426950408889634
 CORES = 2
 QB = 256
-MT = 256
+MT = 512
+NT = 1024
 VMEM_LIMIT = 67043328
 MESH = pl.DeviceIdType.MESH
 F32 = jnp.float32
@@ -58,9 +59,9 @@
 
 
 def main_kernel(n_dev, x_ref, g_ref, p_ref, f_ref, w_ref, wq, wk, wv, wo,
-                h_out, g_out, o_out, gq_out, gk_out, gv_out, a_out, dx_out, dl_out,
-                h_all, g_all, pos, cos_s, sin_s, w3, wo_s, qkv, do_s,
-                res, m_s, li_s, kt_s, vt_s, pt_s, dst_s, a_part, a_recv, dh_part, dh_recv, dl_buf,
+                h_out, g_out, ot_out, gq_out, gk_out, gv_out, a_out, dx_out, dl_out,
+                h_all, g_all, pos, cos_s, sin_s, w3, wo_s, wot_s, qkv, do_s,
+                ot_s, res, m_s, li_s, kt_s, vt_s, pt_s, dst_s, a_part, a_recv, dh_part, dh_recv, cols_s, dl_buf,
                 ssem, rsem, wsem, lsem, xsem, osem, psem, dsem, fsem):
     blk, model = x_ref.shape
     half = blk // 2
@@ -159,9 +160,9 @@
             small(buf, sems, k, me, partner).wait_send()
 
     pl.semaphore_wait(barrier, n_dev - 1)
+    small_send(pos, psem)
     for kind in (1, 4, 2, 3, 0):
         send(0, kind)
-    small_send(pos, psem)
     send(1, 0)
 
     def pass_first(a):
@@ -220,6 +221,8 @@
 
         @pl.when(it == 3)
         def _():
+            for e in range(width // QB):
+                wot_s[:, e * QB:(e + 1) * QB] = wo_s[e * QB:(e + 1) * QB, :].T
             pass_first(0)
             for kind in (1, 4, 2, 3):
                 send(1, kind)
@@ -232,26 +235,36 @@
             from_partner(0, (11, 12))
 
         r = chip_rows(i)
-        y = nn(h_all[r, :], w3[j])
         is_v = j == 2
-        c = jnp.where(is_v, 1.0, cos_s[r, :])
-        s = jnp.where(is_v, 0.0, sin_s[r, :])
-        for n in range(heads):
-            yn = y[:, n * HEAD_DIM:(n + 1) * HEAD_DIM]
-            qkv[j, n, r, :] = (yn * c + swap_pairs(yn) * s).astype(BF16)
+        for part in range(0, heads, 4):
+            y = nn(h_all[r, :], w3[j, :, part * HEAD_DIM:(part + 4) * HEAD_DIM])
+            c = jnp.where(is_v, 1.0, cos_s[r, :])
+            s = jnp.where(is_v, 0.0, sin_s[r, :])
+            for n in range(4):
+                yn = y[:, n * HEAD_DIM:(n + 1) * HEAD_DIM]
+                qkv[j, part + n, r, :] = (yn * c + swap_pairs(yn) * s).astype(BF16)
 
     h_copy = pltpu.make_async_copy(h_all, h_out, lsem.at[0])
     h_copy.start()
 
-    outs = (o_out, gq_out, gk_out, gv_out)
+    outs = (ot_out, gq_out, gk_out, gv_out)
+
+    def slab(a, n):
+        span = pl.ds(pl.multiple_of(core * width + n * HEAD_DIM, HEAD_DIM), HEAD_DIM)
+        return (ot_s.at[n], outs[0].at[span, :]) if a == 0 else (res.at[a - 1, n], outs[a].at[:, span])
 
     def send_head(a, n):
-        cols = pl.ds(pl.multiple_of(core * width + n * HEAD_DIM, HEAD_DIM), HEAD_DIM)
-        pltpu.make_async_copy(res.at[a, n], outs[a].at[:, cols], osem.at[a]).start()
+        src, dst = slab(a, n)
+        pltpu.make_async_copy(src, dst, osem.at[a]).start()
         pltpu.make_async_remote_copy(
-            src_ref=res.at[a, n], dst_ref=outs[a].at[:, cols],
-            send_sem=xsem.at[0, a], recv_sem=xsem.at[1, a],
+            src_ref=src, dst_ref=dst, send_sem=xsem.at[0, a], recv_sem=xsem.at[1, a],
             device_id={"sp": partner}, device_id_type=MESH).start()
+
+    def in_turn(streams):
+        while streams:
+            for g in list(streams):
+                if next(g, None) is None:
+                    streams.remove(g)
 
     c2 = SCALE * LOG2E
     causal = (lax.broadcasted_iota(jnp.int32, (QB, QB), 0)
@@ -264,24 +277,32 @@
         s = nt(qkv[1, n, tile(j), :], qkv[0, n, tile(i), :])
         return jnp.where(causal, s, -jnp.inf) if i == j else s
 
-    @pl.loop(0, heads)
-    def _(n):
-        @pl.when(n == 2)
-        def _():
-            got(1, 0)
-            pass_first(1)
-
-        vt_s[...] = qkv[2, n].T
+    def forward(n, slot):
+        vt = vt_s.at[slot]
+        vt[...] = qkv[2, n].T
         for i in range(nq):
             ss = [scores(n, i, j) for j in range(i + 1)]
+            yield True
             m = functools.reduce(jnp.maximum, [jnp.max(s, axis=0, keepdims=True) for s in ss])
             es = [jnp.exp2((s - m) * c2) for s in ss]
             li = 1.0 / sum(jnp.sum(e, axis=0, keepdims=True) for e in es)
             m_s[n, :, tile(i)] = m
             li_s[n, :, tile(i)] = li
-            o_t = sum(nn(vt_s[:, tile(j)], (e * li).astype(BF16)) for j, e in enumerate(es))
-            res[0, n, tile(i), :] = o_t.T.astype(BF16)
-        send_head(0, n)
+            ps = [(e * li).astype(BF16) for e in es]
+            yield True
+            ot_s[n, :, tile(i)] = sum(nn(vt[:, tile(j)], p) for j, p in enumerate(ps)).astype(BF16)
+            yield True
+
+    @pl.loop(0, heads // 2)
+    def _(t):
+        @pl.when(t == 1)
+        def _():
+            got(1, 0)
+            pass_first(1)
+
+        in_turn([forward(2 * t, 0), forward(2 * t + 1, 1)])
+        send_head(0, 2 * t)
+        send_head(0, 2 * t + 1)
 
     @pl.loop(0, n_chips)
     def _(i):
@@ -296,64 +317,82 @@
             from_partner(1, (11, 12))
 
         r = chip_rows(i)
-        y = nt(g_all[r, :], wo_s[...])
-        for n in range(heads):
-            do_s[n, r, :] = y[:, n * HEAD_DIM:(n + 1) * HEAD_DIM].astype(BF16)
+        for part in range(0, heads, 4):
+            y = nn(g_all[r, :], wot_s[:, part * HEAD_DIM:(part + 4) * HEAD_DIM])
+            for n in range(4):
+                do_s[part + n, r, :] = y[:, n * HEAD_DIM:(n + 1) * HEAD_DIM].astype(BF16)
 
     g_copy = pltpu.make_async_copy(g_all, g_out, lsem.at[1])
     g_copy.start()
-
-    def rows_of(a, r):
-        return jnp.concatenate([res[a, n, r, :] for n in range(heads)], axis=1)
 
     here = pl.ds(pl.multiple_of(chip * rows_chip, rows_chip), rows_chip)
     mine = pl.ds(pl.multiple_of(core * blk, blk), blk)
     theirs = pl.ds(pl.multiple_of(other * blk, blk), blk)
 
-    def swap_part(part, recv, k):
+    def swap_part(src, recv, k):
         return pltpu.make_async_remote_copy(
-            src_ref=part.at[theirs, :], dst_ref=recv,
-            send_sem=fsem.at[0, k], recv_sem=fsem.at[1, k],
+            src_ref=src, dst_ref=recv, send_sem=fsem.at[0, k], recv_sem=fsem.at[1, k],
             device_id={"sp": partner}, device_id_type=MESH)
 
-    a_part[...] = nn(rows_of(0, here), wo_s[...])
-    a_swap = swap_part(a_part, a_recv, 0)
+    o_here = jnp.concatenate([ot_s[n, :, here] for n in range(heads)], axis=0).T
+    for n in range(0, model, NT):
+        a_part[:, n:n + NT] = nn(o_here, wo_s[:, n:n + NT])
+    a_swap = swap_part(a_part.at[theirs, :], a_recv, 0)
     a_swap.start()
 
-    @pl.loop(0, heads)
-    def _(n):
-        kt_s[...] = qkv[1, n].T
-        for i in range(nq):
+    def at(j, i):
+        return i * (i + 1) // 2 + j
+
+    def backward(n, slot):
+        kt, pt, dst = kt_s.at[slot], pt_s.at[slot], dst_s.at[slot]
+        kt[...] = qkv[1, n].T
+        for i in reversed(range(nq)):
             q_i, do_i = qkv[0, n, tile(i), :], do_s[n, tile(i), :]
+            ss = [scores(n, i, j) for j in range(i + 1)]
+            dps = [nt(qkv[2, n, tile(j), :], do_i) for j in range(i + 1)]
+            yield True
             m, li = m_s[n, :, tile(i)], li_s[n, :, tile(i)]
-            ps, dps = [], []
-            rdot = 0.0
+            ps = [jnp.exp2((s - m) * c2) * li for s in ss]
+            rdot = sum(jnp.sum(p * dp, axis=0, keepdims=True) for p, dp in zip(ps, dps))
             for j in range(i + 1):
-                p = jnp.exp2((scores(n, i, j) - m) * c2) * li
-                dp = nt(qkv[2, n, tile(j), :], do_i)
-                rdot = rdot + jnp.sum(p * dp, axis=0, keepdims=True)
-                pt_s[tile(j), tile(i)] = p.astype(BF16)
-                ps.append(p)
-                dps.append(dp)
-            for j in range(i + 1):
-                dst_s[tile(j), tile(i)] = (ps[j] * (dps[j] - rdot) * SCALE).astype(BF16)
-            dq = nn(kt_s[:, :(i + 1) * QB], dst_s[:(i + 1) * QB, tile(i)]).T.astype(BF16).astype(F32)
-            res[1, n, tile(i), :] = (dq * cos_s[tile(i), :] - swap_pairs(dq) * sin_s[tile(i), :]).astype(BF16)
-        for j in range(nq):
-            dk = nn(dst_s[tile(j), j * QB:], qkv[0, n, j * QB:, :]).astype(BF16).astype(F32)
-            res[2, n, tile(j), :] = (dk * cos_s[tile(j), :] - swap_pairs(dk) * sin_s[tile(j), :]).astype(BF16)
-            res[3, n, tile(j), :] = nn(pt_s[tile(j), j * QB:], do_s[n, j * QB:, :]).astype(BF16)
+                pt[at(j, i)] = ps[j].astype(BF16)
+                dst[at(j, i)] = (ps[j] * (dps[j] - rdot) * SCALE).astype(BF16)
+            yield True
+            dq = sum(nn(kt[:, tile(j)], dst[at(j, i)]) for j in range(i + 1)).T.astype(BF16).astype(F32)
+            c, s = cos_s[tile(i), :], sin_s[tile(i), :]
+            res[0, n, tile(i), :] = (dq * c - swap_pairs(dq) * s).astype(BF16)
+            dk = sum(nn(dst[at(i, k)], qkv[0, n, tile(k), :]) for k in range(i, nq)).astype(BF16).astype(F32)
+            res[1, n, tile(i), :] = (dk * c - swap_pairs(dk) * s).astype(BF16)
+            res[2, n, tile(i), :] = sum(nn(pt[at(i, k)], do_s[n, tile(k), :]) for k in range(i, nq)).astype(BF16)
+            yield True
+
+    @pl.loop(0, heads // 2)
+    def _(t):
+        in_turn([backward(2 * t, 0), backward(2 * t + 1, 1)])
         for a in (1, 2, 3):
-            send_head(a, n)
-
-    dh_part[...] = sum(nt(rows_of(j + 1, here), w3[j]) for j in range(3))
-    dh_swap = swap_part(dh_part, dh_recv, 1)
+            send_head(a, 2 * t)
+            send_head(a, 2 * t + 1)
+
+    def cols_of(j):
+        return jnp.concatenate([res[j, n, here, :] for n in range(heads)], axis=1).T
+
+    for j in range(3):
+        cols_s[j] = cols_of(j)
+
+    @pl.loop(0, model // MT)
+    def _(d):
+        r = pl.ds(pl.multiple_of(d * MT, MT), MT)
+        dh_t = sum(nn(w3[j, r, :], cols_s[j]) for j in range(3))
+        for k in range(CORES):
+            dh_part[k, r, :] = dh_t[:, k * blk:(k + 1) * blk]
+
+    dh_swap = swap_part(dh_part.at[other], dh_recv, 1)
     dh_swap.start()
     a_swap.wait()
     a_out[...] = (a_part[mine, :] + a_recv[...]).astype(BF16)
     xhat, rstd = normalize(x_ref[...])
     dh_swap.wait()
-    dh = dh_part[mine, :] + dh_recv[...]
+    dh = (dh_part[core] + dh_recv[...]).T
     dl_buf[me] = jnp.sum(dh * xhat, axis=0, keepdims=True)
     small_send(dl_buf, dsem)
     dy = dh * ln_w
@@ -365,13 +404,14 @@
     for a in range(2):
         for kind, (block, piece, to) in sends.items():
             copy(a, kind, block, piece, to).wait_send()
-    my_cols = pl.ds(pl.multiple_of(core * width, width), width)
-    their_cols = pl.ds(pl.multiple_of(other * width, width), width)
+    my_span = pl.ds(pl.multiple_of(core * width, width), width)
+    their_span = pl.ds(pl.multiple_of(other * width, width), width)
     for a in range(4):
-        pltpu.make_async_copy(outs[a].at[:, my_cols], outs[a].at[:, my_cols], osem.at[a]).wait()
+        sent = outs[a].at[my_span, :] if a == 0 else outs[a].at[:, my_span]
+        came = outs[a].at[their_span, :] if a == 0 else outs[a].at[:, their_span]
+        pltpu.make_async_copy(sent, sent, osem.at[a]).wait()
         done = pltpu.make_async_remote_copy(
-            src_ref=outs[a].at[:, my_cols], dst_ref=outs[a].at[:, their_cols],
-            send_sem=xsem.at[0, a], recv_sem=xsem.at[1, a],
+            src_ref=sent, dst_ref=came, send_sem=xsem.at[0, a], recv_sem=xsem.at[1, a],
             device_id={"sp": partner}, device_id_type=MESH)
         done.wait_send()
         done.wait_recv()
@@ -387,6 +427,7 @@
     seq = n_dev * blk
     width = w_q.shape[1] // CORES
     heads = width // HEAD_DIM
+    pairs = (seq // QB) * (seq // QB + 1) // 2
     vm = pl.BlockSpec(memory_space=pltpu.VMEM)
     hbm = pl.BlockSpec(memory_space=pl.ANY)
     full = jax.ShapeDtypeStruct((seq, model), BF16)
@@ -395,7 +436,7 @@
     freq = jnp.repeat(ROPE_BASE ** (-jnp.arange(0, HEAD_DIM, 2, dtype=F32) / HEAD_DIM), 2)[None, :]
     return pl.pallas_call(
         functools.partial(main_kernel, n_dev),
-        out_shape=(full, full, wide, wide, wide, wide, rows, rows, jax.ShapeDtypeStruct((model,), BF16)),
+        out_shape=(full, full, jax.ShapeDtypeStruct((w_q.shape[1], seq), BF16), wide, wide, wide, rows, rows, jax.ShapeDtypeStruct((model,), BF16)),
         in_specs=[vm] * 5 + [hbm] * 4,
         out_specs=[hbm] * 6 + [vm] * 3,
         scratch_shapes=[
@@ -406,19 +447,22 @@
             pltpu.VMEM((seq, HEAD_DIM), F32),
             pltpu.VMEM((3, model, width), BF16),
             pltpu.VMEM((width, model), BF16),
+            pltpu.VMEM((model, width), BF16),
             pltpu.VMEM((3, heads, seq, HEAD_DIM), BF16),
             pltpu.VMEM((heads, seq, HEAD_DIM), BF16),
-            pltpu.VMEM((4, heads, seq, HEAD_DIM), BF16),
+            pltpu.VMEM((heads, HEAD_DIM, seq), BF16),
+            pltpu.VMEM((3, heads, seq, HEAD_DIM), BF16),
             pltpu.VMEM((heads, 1, seq), F32),
             pltpu.VMEM((heads, 1, seq), F32),
-            pltpu.VMEM((HEAD_DIM, seq), BF16),
-            pltpu.VMEM((HEAD_DIM, seq), BF16),
-            pltpu.VMEM((seq, seq), BF16),
-            pltpu.VMEM((seq, seq), BF16),
+            pltpu.VMEM((2, HEAD_DIM, seq), BF16),
+            pltpu.VMEM((2, HEAD_DIM, seq), BF16),
+            pltpu.VMEM((2, pairs, QB, QB), BF16),
+            pltpu.VMEM((2, pairs, QB, QB), BF16),
             pltpu.VMEM((CORES * blk, model), F32),
             pltpu.VMEM((blk, model), F32),
-            pltpu.VMEM((CORES * blk, model), F32),
-            pltpu.VMEM((blk, model), F32),
+            pltpu.VMEM((CORES, model, blk), F32),
+            pltpu.VMEM((model, blk), F32),
+            pltpu.VMEM((3, width, CORES * blk), BF16),
             pltpu.VMEM((n_dev, 1, model), F32),
             pltpu.SemaphoreType.DMA((2, 13)),
             pltpu.SemaphoreType.DMA((2, 13)),
@@ -436,55 +480,111 @@
     )(hidden, d_attn, positions, freq, ln_weight, w_q, w_k, w_v, w_o)
 
 
-def grad_kernel(h_ref, o_ref, gq, gk, gv, g, dq_ref, dk_ref, dv_ref, do_ref, rhs, sem):
-    w, m = pl.program_id(0), pl.program_id(1)
-
-    def load(k):
-        src = (gq, gk, gv, g)[k]
-        return pltpu.make_async_copy(src, rhs.at[k % 2], sem.at[k % 2])
-
-    for k in range(4):
-        @pl.when((w == k) & (m == 0))
-        def _():
-            if k == 0:
-                load(0).start()
-            load(k).wait()
-            if k < 3:
-                load(k + 1).start()
-
-    def tn(a):
-        b = rhs[lax.rem(w, 2)]
-        return lax.dot_general(a, b, (((0,), (0,)), ((), ())), preferred_element_type=F32).astype(BF16)
-
-    for k, out in enumerate((dq_ref, dk_ref, dv_ref, do_ref)):
-        @pl.when(w == k)
-        def _():
-            out[...] = tn(o_ref[...] if k == 3 else h_ref[...])
-
-
-def run_grads(h, o, gq, gk, gv, g):
+def grad_kernel(ot, g, h, gq, gk, gv, a_in, dx_in, dl_in, dq_out, dk_out, dv_out, do_out, a_out, dx_out, dl_out,
+                ot_v, g_v, h_v, ht_v, g3, out_v, a_v, dx_v, sem, msem, usem):
+    tiles = ot.shape[0] // MT
+    wide = g.shape[1]
+    outs = (dq_out, dk_out, dv_out)
+
+    def rows(m):
+        return pl.ds(pl.multiple_of(m * MT, MT), MT)
+
+    ot_loads = [pltpu.make_async_copy(ot.at[rows(m), :], ot_v.at[rows(m), :], msem.at[m]) for m in range(tiles)]
+    g_load = pltpu.make_async_copy(g, g_v, sem.at[0])
+    h_load = pltpu.make_async_copy(h, h_v, sem.at[1])
+    g3_loads = [pltpu.make_async_copy(x, g3.at[k], sem.at[2 + k]) for k, x in enumerate((gq, gk, gv))]
+    small_in = [pltpu.make_async_copy(a_in, a_v, sem.at[5]), pltpu.make_async_copy(dx_in, dx_v, sem.at[6])]
+    small_out = [pltpu.make_async_copy(a_v, a_out, sem.at[5]), pltpu.make_async_copy(dx_v, dx_out, sem.at[6])]
+    ot_loads[0].start()
+    g_load.start()
+    h_load.start()
+    for c in ot_loads[1:] + g3_loads + small_in:
+        c.start()
+    dl_out[...] = dl_in[...]
+
+    def store(slot, out, m):
+        return pltpu.make_async_copy(out_v.at[slot], out.at[rows(m), :], usem.at[slot])
+
+    def product(slot, a, b):
+        for n in range(0, wide, NT):
+            out_v[slot, :, n:n + NT] = nn(a, b[:, n:n + NT]).astype(BF16)
+
+    def turn(m):
+        ht_v[rows(m), :] = h_v[:, rows(m)].T
+
+    for m in range(tiles):
+        ot_loads[m].wait()
+        if m == 0:
+            g_load.wait()
+        if m == 1:
+            h_load.wait()
+        if m >= 2:
+            store(m % 2, do_out, m - 2).wait()
+        if m >= 1:
+            turn(m - 1)
+        product(m % 2, ot_v[m * MT:(m + 1) * MT, :], g_v)
+        store(m % 2, do_out, m).start()
+
+    turn(tiles - 1)
+    for c in small_in:
+        c.wait()
+    for c in small_out:
+        c.start()
+
+    @pl.loop(0, 3 * tiles)
+    def _(it):
+        k, m, slot = it // tiles, lax.rem(it, tiles), lax.rem(it, 2)
+        for j in range(3):
+            @pl.when(it == j * tiles)
+            def _():
+                g3_loads[j].wait()
+
+        store(slot, do_out, 0).wait()
+        product(slot, ht_v[rows(m), :], g3.at[k])
+        for j in range(3):
+            @pl.when(k == j)
+            def _():
+                store(slot, outs[j], m).start()
+
+    for slot in range(2):
+        store(slot, do_out, 0).wait()
+    for c in small_out:
+        c.wait()
+
+
+def run_grads(h, g, ot, gq, gk, gv, attn_out, d_hid, d_lnw):
     seq, model = h.shape
     wide = gq.shape[1]
-    steps = model // MT
+    tiles = model // MT
     hbm = pl.BlockSpec(memory_space=pl.ANY)
-
-    def out_spec(k):
-        return pl.BlockSpec((MT, wide), lambda w, m: (jnp.where(w == k, m, jnp.where(w < k, 0, steps - 1)), 0))
+    vm = pl.BlockSpec(memory_space=pltpu.VMEM)
+    grad = jax.ShapeDtypeStruct((model, wide), BF16)
+
+    def like(a):
+        return jax.ShapeDtypeStruct(a.shape, a.dtype)
 
     return pl.pallas_call(
         grad_kernel,
-        grid=(4, steps),
-        out_shape=[jax.ShapeDtypeStruct((model, wide), BF16)] * 4,
-        in_specs=[
-            pl.BlockSpec((seq, MT), lambda w, m: (0, jnp.where(w < 3, m, steps - 1))),
-            pl.BlockSpec((seq, MT), lambda w, m: (0, jnp.where(w < 3, 0, m))),
-            hbm, hbm, hbm, hbm],
-        out_specs=[out_spec(k) for k in range(4)],
-        scratch_shapes=[pltpu.VMEM((2, seq, wide), BF16), pltpu.SemaphoreType.DMA((2,))],
-        compiler_params=pltpu.CompilerParams(
-            dimension_semantics=("arbitrary", "arbitrary"), vmem_limit_bytes=VMEM_LIMIT),
+        out_shape=[grad, grad, grad, jax.ShapeDtypeStruct((wide, model), BF16),
+                   like(attn_out), like(d_hid), like(d_lnw)],
+        in_specs=[hbm] * 8 + [vm],
+        out_specs=[hbm] * 6 + [vm],
+        scratch_shapes=[
+            pltpu.VMEM((wide, seq), BF16),
+            pltpu.VMEM((seq, model), BF16),
+            pltpu.VMEM((seq, model), BF16),
+            pltpu.VMEM((model, seq), BF16),
+            pltpu.VMEM((3, seq, wide), BF16),
+            pltpu.VMEM((2, MT, wide), BF16),
+            pltpu.VMEM(attn_out.shape, BF16),
+            pltpu.VMEM(d_hid.shape, BF16),
+            pltpu.SemaphoreType.DMA((7,)),
+            pltpu.SemaphoreType.DMA((tiles,)),
+            pltpu.SemaphoreType.DMA((2,)),
+        ],
+        compiler_params=pltpu.CompilerParams(vmem_limit_bytes=VMEM_LIMIT),
         name="weight_grads",
-    )(h, o, gq, gk, gv, g)
+    )(ot, g, h, gq, gk, gv, attn_out, d_hid, d_lnw)
 
 
 def solution(mesh):
@@ -494,9 +594,10 @@
     grad_spec = P('dp', None)
 
     def local_step(hidden, positions, d_attn, ln_weight, w_q, w_k, w_v, w_o):
-        h, g, o, gq, gk, gv, attn_out, d_hid, d_lnw = run_main(
+        h, g, ot, gq, gk, gv, attn_out, d_hid, d_lnw = run_main(
             n_dev, hidden, d_attn, positions, ln_weight, w_q, w_k, w_v, w_o)
-        return (attn_out, d_hid, d_lnw, *run_grads(h, o, gq, gk, gv, g))
+        dwq, dwk, dwv, dwo, attn_out, d_hid, d_lnw = run_grads(h, g, ot, gq, gk, gv, attn_out, d_hid, d_lnw)
+        return attn_out, d_hid, d_lnw, dwq, dwk, dwv, dwo
 
     return jax.shard_map(local_step, mesh=mesh,
                          in_specs=(row_spec, P(('dp', 'sp')), row_spec, P(None), full_spec, full_spec, full_spec, full_spec),

time: 164 us -> 136 us (0.83)
  Pallas kernels: 157 us -> 134 us
  local copies, waits for them, and re-layouts: 5.77 us -> 0.73 us
    pallas_call x1, Pallas kernels: 105 us -> 88.8 us  [run_main(): pl.pallas_call(functools.partial(main_kernel, n_dev), out_shape=(full, fu...]
    pallas_call x1, Pallas kernels: 51.3 us -> 45.2 us  [run_grads(): pl.pallas_call(grad_kernel, out_shape=[grad, grad, grad, jax.ShapeDtypeSt...]
    unnamed x3 -> x0, local copies, waits for them, and re-layouts: 5.03 us -> none
where the time goes in v1:
time: 136 us
  Pallas kernels  134 us (99%)
    pallas_call x1, Pallas kernels, run_main(): pl.pallas_call(functools.partial(main_kernel, n_dev), out_shape=(full, fu...  88.8 us
    pallas_call x1, Pallas kernels, run_grads(): pl.pallas_call(grad_kernel, out_shape=[grad, grad, grad, jax.ShapeDtypeSt...  45.2 us

profile of v1, /device:TPU:81, one launch (start us, length us, event | category | flops | bytes accessed | tf_op | source)
XLA Modules:
  0.0 135.5 jit_solution(6731984995391109156)
XLA Ops:
  0.6 0.1 broadcast_in_dim.3
  0.7 0.7 broadcast_in_dim_reshape.3.f_ref
  1.4 88.8 %gather_attention.1 = (bf16[1024,2048]{1,0:T(8,128)(2,1)}, bf16[1024,2048]{1,0:T(8,128)(2,1)}, bf16[2048,1024]{1,0:T(8,128)(2,1)}, bf16[1024,2048]{1,0:T(8,128)(...) custom-call(bf16[128,2048]{1,0:T(8,128)(2,1)} %x_ref.1, ...), custom_call_target="tpu_custom_call" | custom-call | tf_op jit(solution)/shard_map/gather_attention/pallas_call | solution.py:437
  90.2 45.2 %weight_grads.1 = (bf16[2048,2048]{1,0:T(8,128)(2,1)}, bf16[2048,2048]{1,0:T(8,128)(2,1)}, bf16[2048,2048]{1,0:T(8,128)(2,1)}, bf16[2048,2048]{1,0:T(8,128)(2,1)...) custom-call(bf16[2048,1024]{1,0:T(8,128)(2,1)} %get-tuple-element.23.ot, ...), custom_call_target="tpu_custom_call" | custom-call | tf_op jit(solution)/shard_map/weight_grads/pallas_call | solution.py:566
  (1 shorter events, 0.0 us)

commit v2 on v1

--- a/solution.py
+++ b/solution.py
@@ -59,7 +59,7 @@
 
 
 def main_kernel(n_dev, x_ref, g_ref, p_ref, f_ref, w_ref, wq, wk, wv, wo,
-                h_out, g_out, ot_out, gq_out, gk_out, gv_out, a_out, dx_out, dl_out,
+                ht_out, dwo_out, gq_out, gk_out, dwv_out, a_out, dx_out, dl_out,
                 h_all, g_all, pos, cos_s, sin_s, w3, wo_s, wot_s, qkv, do_s,
                 ot_s, res, m_s, li_s, kt_s, vt_s, pt_s, dst_s, a_part, a_recv, dh_part, dh_recv, cols_s, dl_buf,
                 ssem, rsem, wsem, lsem, xsem, osem, psem, dsem, fsem):
@@ -208,57 +208,83 @@
             cos_s[r, :] = cos
             sin_s[r, :] = jnp.where(even, -sin, sin)
 
-    @pl.loop(0, 3 * n_chips)
-    def _(it):
-        i, j = it // 3, lax.rem(it, 3)
-
-        @pl.when(it == 0)
+    def project_do(r):
+        for part in range(0, heads, 4):
+            y = nn(g_all[r, :], wot_s[:, part * HEAD_DIM:(part + 4) * HEAD_DIM])
+            for n in range(4):
+                do_s[part + n, r, :] = y[:, n * HEAD_DIM:(n + 1) * HEAD_DIM].astype(BF16)
+
+    def job_rows(i):
+        mid, late = (lax.rem(i, 3) + 1) // 2, i // 2
+        runs = []
+        for k in range(4):
+            beside = (n_chips - 1, half * late + blk * k) if k < 2 else (1, half * (1 - late) + blk * (k - 2))
+            step = (1 - mid) * (i // 3) * far + mid * beside[0]
+            row = lax.rem(chip + step, n_chips) * rows_chip + (1 - mid) * half * k + mid * beside[1]
+            runs.append(pl.ds(pl.multiple_of(row, half), half))
+        return runs
+
+    @pl.loop(0, n_chips)
+    def _(i):
+        @pl.when(i == 0)
         def _():
             fill_tables()
             got(0, 0)
             for c in wcopies:
                 c.wait()
 
-        @pl.when(it == 3)
+        @pl.when(i == 1)
         def _():
             for e in range(width // QB):
                 wot_s[:, e * QB:(e + 1) * QB] = wo_s[e * QB:(e + 1) * QB, :].T
+            got(1, 0)
+            project_do(chip_rows(0))
             pass_first(0)
             for kind in (1, 4, 2, 3):
                 send(1, kind)
+            from_partner(0, (7, 10))
+
+        @pl.when(i == 2)
+        def _():
             pass_second(0)
-            from_partner(0, (7, 8, 9, 10))
-
-        @pl.when(it == 9)
+            from_partner(0, (8, 9))
+
+        @pl.when(i == 3)
         def _():
             pass_far(0)
             from_partner(0, (11, 12))
 
-        r = chip_rows(i)
-        is_v = j == 2
-        for part in range(0, heads, 4):
-            y = nn(h_all[r, :], w3[j, :, part * HEAD_DIM:(part + 4) * HEAD_DIM])
-            c = jnp.where(is_v, 1.0, cos_s[r, :])
-            s = jnp.where(is_v, 0.0, sin_s[r, :])
-            for n in range(4):
-                yn = y[:, n * HEAD_DIM:(n + 1) * HEAD_DIM]
-                qkv[j, part + n, r, :] = (yn * c + swap_pairs(yn) * s).astype(BF16)
-
-    h_copy = pltpu.make_async_copy(h_all, h_out, lsem.at[0])
-    h_copy.start()
-
-    outs = (ot_out, gq_out, gk_out, gv_out)
-
-    def slab(a, n):
-        span = pl.ds(pl.multiple_of(core * width + n * HEAD_DIM, HEAD_DIM), HEAD_DIM)
-        return (ot_s.at[n], outs[0].at[span, :]) if a == 0 else (res.at[a - 1, n], outs[a].at[:, span])
-
-    def send_head(a, n):
-        src, dst = slab(a, n)
+        runs = job_rows(i)
+
+        def rows_of(ref):
+            return jnp.concatenate([ref[r, :] for r in runs], axis=0)
+
+        x = rows_of(h_all)
+        c, s = rows_of(cos_s), rows_of(sin_s)
+        for j in range(3):
+            for part in range(0, heads, 4):
+                y = nn(x, w3[j, :, part * HEAD_DIM:(part + 4) * HEAD_DIM])
+                for n in range(4):
+                    yn = y[:, n * HEAD_DIM:(n + 1) * HEAD_DIM]
+                    yn = (yn if j == 2 else yn * c + swap_pairs(yn) * s).astype(BF16)
+                    for k, r in enumerate(runs):
+                        qkv[j, part + n, r, :] = yn[k * half:(k + 1) * half]
+
+
+    outs = (dwo_out, gq_out, gk_out, dwv_out)
+    my_col = core * width
+
+    def give(a, src, dst):
         pltpu.make_async_copy(src, dst, osem.at[a]).start()
         pltpu.make_async_remote_copy(
             src_ref=src, dst_ref=dst, send_sem=xsem.at[0, a], recv_sem=xsem.at[1, a],
             device_id={"sp": partner}, device_id_type=MESH).start()
+
+    def head_cols(n):
+        return pl.ds(pl.multiple_of(my_col + n * HEAD_DIM, HEAD_DIM), HEAD_DIM)
+
+    def rows_tile(m):
+        return pl.ds(pl.multiple_of(m * MT, MT), MT)
 
     def in_turn(streams):
         while streams:
@@ -297,33 +323,9 @@
     def _(t):
         @pl.when(t == 1)
         def _():
-            got(1, 0)
             pass_first(1)
 
         in_turn([forward(2 * t, 0), forward(2 * t + 1, 1)])
-        send_head(0, 2 * t)
-        send_head(0, 2 * t + 1)
-
-    @pl.loop(0, n_chips)
-    def _(i):
-        @pl.when(i == 1)
-        def _():
-            pass_second(1)
-            from_partner(1, (7, 8, 9, 10))
-
-        @pl.when(i == 3)
-        def _():
-            pass_far(1)
-            from_partner(1, (11, 12))
-
-        r = chip_rows(i)
-        for part in range(0, heads, 4):
-            y = nn(g_all[r, :], wot_s[:, part * HEAD_DIM:(part + 4) * HEAD_DIM])
-            for n in range(4):
-                do_s[part + n, r, :] = y[:, n * HEAD_DIM:(n + 1) * HEAD_DIM].astype(BF16)
-
-    g_copy = pltpu.make_async_copy(g_all, g_out, lsem.at[1])
-    g_copy.start()
 
     here = pl.ds(pl.multiple_of(chip * rows_chip, rows_chip), rows_chip)
     mine = pl.ds(pl.multiple_of(core * blk, blk), blk)
@@ -334,11 +336,40 @@
             src_ref=src, dst_ref=recv, send_sem=fsem.at[0, k], recv_sem=fsem.at[1, k],
             device_id={"sp": partner}, device_id_type=MESH)
 
-    o_here = jnp.concatenate([ot_s[n, :, here] for n in range(heads)], axis=0).T
-    for n in range(0, model, NT):
-        a_part[:, n:n + NT] = nn(o_here, wo_s[:, n:n + NT])
     a_swap = swap_part(a_part.at[theirs, :], a_recv, 0)
-    a_swap.start()
+
+    @pl.loop(1, n_chips)
+    def _(i):
+        @pl.when(i == 1)
+        def _():
+            pass_second(1)
+            from_partner(1, (7, 8, 9, 10))
+
+        @pl.when(i == 3)
+        def _():
+            o_here = jnp.concatenate([ot_s[n, :, here] for n in range(heads)], axis=0).T
+            for n in range(0, model, NT):
+                a_part[:, n:n + NT] = nn(o_here, wo_s[:, n:n + NT])
+            a_swap.start()
+            pass_far(1)
+            from_partner(1, (11, 12))
+
+        project_do(chip_rows(i))
+
+    for kind, (block, piece, to) in sends.items():
+        copy(0, kind, block, piece, to).wait_send()
+    for e in range(0, model, QB):
+        wot_s[e:e + QB, :] = h_all[:, e:e + QB].T
+    ht_copy = pltpu.make_async_copy(wot_s, ht_out, lsem.at[0])
+    ht_copy.start()
+
+    @pl.loop(0, width // MT)
+    def _(m):
+        per = MT // HEAD_DIM
+        o_t = jnp.concatenate([ot_s[m * per + n] for n in range(per)], axis=0)
+        for n in range(0, model, NT):
+            h_all[rows_tile(m), n:n + NT] = nn(o_t, g_all[:, n:n + NT]).astype(BF16)
+        give(0, h_all.at[rows_tile(m), :], dwo_out.at[pl.ds(pl.multiple_of(my_col + m * MT, MT), MT), :])
 
     def at(j, i):
         return i * (i + 1) // 2 + j
@@ -348,15 +379,22 @@
         kt[...] = qkv[1, n].T
         for i in reversed(range(nq)):
             q_i, do_i = qkv[0, n, tile(i), :], do_s[n, tile(i), :]
-            ss = [scores(n, i, j) for j in range(i + 1)]
-            dps = [nt(qkv[2, n, tile(j), :], do_i) for j in range(i + 1)]
+            m, li = m_s[n, :, tile(i)], li_s[n, :, tile(i)]
+            ps, ts, rdot = [], [], 0.0
+            s, dp = scores(n, i, 0), nt(qkv[2, n, tile(0), :], do_i)
+            for j in range(i + 1):
+                yield True
+                p = jnp.exp2((s - m) * c2) * li
+                t = p * dp
+                rdot = rdot + jnp.sum(t, axis=0, keepdims=True)
+                pt[at(j, i)] = p.astype(BF16)
+                ps.append(p)
+                ts.append(t)
+                if j < i:
+                    s, dp = scores(n, i, j + 1), nt(qkv[2, n, tile(j + 1), :], do_i)
             yield True
-            m, li = m_s[n, :, tile(i)], li_s[n, :, tile(i)]
-            ps = [jnp.exp2((s - m) * c2) * li for s in ss]
-            rdot = sum(jnp.sum(p * dp, axis=0, keepdims=True) for p, dp in zip(ps, dps))
             for j in range(i + 1):
-                pt[at(j, i)] = ps[j].astype(BF16)
-                dst[at(j, i)] = (ps[j] * (dps[j] - rdot) * SCALE).astype(BF16)
+                dst[at(j, i)] = ((ts[j] - ps[j] * rdot) * SCALE).astype(BF16)
             yield True
             dq = sum(nn(kt[:, tile(j)], dst[at(j, i)]) for j in range(i + 1)).T.astype(BF16).astype(F32)
             c, s = cos_s[tile(i), :], sin_s[tile(i), :]
@@ -369,9 +407,9 @@
     @pl.loop(0, heads // 2)
     def _(t):
         in_turn([backward(2 * t, 0), backward(2 * t + 1, 1)])
-        for a in (1, 2, 3):
-            send_head(a, 2 * t)
-            send_head(a, 2 * t + 1)
+        for a in (1, 2):
+            for n in (2 * t, 2 * t + 1):
+                give(a, res.at[a - 1, n], outs[a].at[:, head_cols(n)])
 
     def cols_of(j):
         return jnp.concatenate([res[j, n, here, :] for n in range(heads)], axis=1).T
@@ -388,22 +426,38 @@
 
     dh_swap = swap_part(dh_part.at[other], dh_recv, 1)
     dh_swap.start()
-    a_swap.wait()
-    a_out[...] = (a_part[mine, :] + a_recv[...]).astype(BF16)
-    xhat, rstd = normalize(x_ref[...])
-    dh_swap.wait()
-    dh = (dh_part[core] + dh_recv[...]).T
-    dl_buf[me] = jnp.sum(dh * xhat, axis=0, keepdims=True)
-    small_send(dl_buf, dsem)
-    dy = dh * ln_w
-    dx = dy - jnp.mean(dy, axis=-1, keepdims=True) - xhat * jnp.mean(dy * xhat, axis=-1, keepdims=True)
-    dx_out[...] = (dx * rstd).astype(BF16)
-
-    h_copy.wait()
-    g_copy.wait()
-    for a in range(2):
-        for kind, (block, piece, to) in sends.items():
-            copy(a, kind, block, piece, to).wait_send()
+
+    def finish_rows():
+        a_swap.wait()
+        a_out[...] = (a_part[mine, :] + a_recv[...]).astype(BF16)
+        xhat, rstd = normalize(x_ref[...])
+        dh_swap.wait()
+        dh = (dh_part[core] + dh_recv[...]).T
+        dl_buf[me] = jnp.sum(dh * xhat, axis=0, keepdims=True)
+        small_send(dl_buf, dsem)
+        dy = dh * ln_w
+        dx = dy - jnp.mean(dy, axis=-1, keepdims=True) - xhat * jnp.mean(dy * xhat, axis=-1, keepdims=True)
+        dx_out[...] = (dx * rstd).astype(BF16)
+
+    @pl.loop(0, model // MT)
+    def _(m):
+        @pl.when(m == 2)
+        def _():
+            finish_rows()
+
+        per = seq // MT
+        place = pl.ds(pl.multiple_of(lax.rem(m, per) * MT, MT), MT)
+        for part in range(0, heads, 4):
+            gv = jnp.concatenate([res[2, part + n] for n in range(4)], axis=1)
+            y = nn(wot_s[rows_tile(m), :], gv).astype(BF16)
+            for n in range(4):
+                qkv[m // per, part + n, place, :] = y[:, n * HEAD_DIM:(n + 1) * HEAD_DIM]
+        for n in range(heads):
+            give(3, qkv.at[m // per, n, place, :], dwv_out.at[rows_tile(m), head_cols(n)])
+
+    ht_copy.wait()
+    for kind, (block, piece, to) in sends.items():
+        copy(1, kind, block, piece, to).wait_send()
     my_span = pl.ds(pl.multiple_of(core * width, width), width)
     their_span = pl.ds(pl.multiple_of(other * width, width), width)
     for a in range(4):
@@ -430,15 +484,16 @@
     pairs = (seq // QB) * (seq // QB + 1) // 2
     vm = pl.BlockSpec(memory_space=pltpu.VMEM)
     hbm = pl.BlockSpec(memory_space=pl.ANY)
-    full = jax.ShapeDtypeStruct((seq, model), BF16)
-    wide = jax.ShapeDtypeStruct((seq, w_q.shape[1]), BF16)
+    full = w_q.shape[1]
+    wide = jax.ShapeDtypeStruct((seq, full), BF16)
     rows = jax.ShapeDtypeStruct((blk, model), BF16)
     freq = jnp.repeat(ROPE_BASE ** (-jnp.arange(0, HEAD_DIM, 2, dtype=F32) / HEAD_DIM), 2)[None, :]
     return pl.pallas_call(
         functools.partial(main_kernel, n_dev),
-        out_shape=(full, full, jax.ShapeDtypeStruct((w_q.shape[1], seq), BF16), wide, wide, wide, rows, rows, jax.ShapeDtypeStruct((model,), BF16)),
+        out_shape=(jax.ShapeDtypeStruct((model, seq), BF16), jax.ShapeDtypeStruct((full, model), BF16),
+                   wide, wide, jax.ShapeDtypeStruct((model, full), BF16), rows, rows, jax.ShapeDtypeStruct((model,), BF16)),
         in_specs=[vm] * 5 + [hbm] * 4,
-        out_specs=[hbm] * 6 + [vm] * 3,
+        out_specs=[hbm] * 5 + [vm] * 3,
         scratch_shapes=[
             pltpu.VMEM((seq, model), BF16),
             pltpu.VMEM((seq, model), BF16),
@@ -467,7 +522,7 @@
             pltpu.SemaphoreType.DMA((2, 13)),
             pltpu.SemaphoreType.DMA((2, 13)),
             pltpu.SemaphoreType.DMA((4,)),
-            pltpu.SemaphoreType.DMA((2,)),
+            pltpu.SemaphoreType.DMA((1,)),
             pltpu.SemaphoreType.DMA((2, 4)),
             pltpu.SemaphoreType.DMA((4,)),
             pltpu.SemaphoreType.DMA((2, n_dev)),
@@ -480,111 +535,117 @@
     )(hidden, d_attn, positions, freq, ln_weight, w_q, w_k, w_v, w_o)
 
 
-def grad_kernel(ot, g, h, gq, gk, gv, a_in, dx_in, dl_in, dq_out, dk_out, dv_out, do_out, a_out, dx_out, dl_out,
-                ot_v, g_v, h_v, ht_v, g3, out_v, a_v, dx_v, sem, msem, usem):
-    tiles = ot.shape[0] // MT
-    wide = g.shape[1]
-    outs = (dq_out, dk_out, dv_out)
-
-    def rows(m):
-        return pl.ds(pl.multiple_of(m * MT, MT), MT)
-
-    ot_loads = [pltpu.make_async_copy(ot.at[rows(m), :], ot_v.at[rows(m), :], msem.at[m]) for m in range(tiles)]
-    g_load = pltpu.make_async_copy(g, g_v, sem.at[0])
-    h_load = pltpu.make_async_copy(h, h_v, sem.at[1])
-    g3_loads = [pltpu.make_async_copy(x, g3.at[k], sem.at[2 + k]) for k, x in enumerate((gq, gk, gv))]
-    small_in = [pltpu.make_async_copy(a_in, a_v, sem.at[5]), pltpu.make_async_copy(dx_in, dx_v, sem.at[6])]
-    small_out = [pltpu.make_async_copy(a_v, a_out, sem.at[5]), pltpu.make_async_copy(dx_v, dx_out, sem.at[6])]
-    ot_loads[0].start()
-    g_load.start()
-    h_load.start()
-    for c in ot_loads[1:] + g3_loads + small_in:
-        c.start()
-    dl_out[...] = dl_in[...]
+def grad_kernel(ht, gq, gk, dwo_in, dwv_in, a_in, dx_in, dl_in,
+                dq_out, dk_out, dwo_out, dwv_out, a_out, dx_out, dl_out,
+                ht_v, g2, out_v, dwo_v, dwv_v, a_v, dx_v, hsem, gsem, usem, isem, osem, rsem):
+    tiles = ht.shape[0] // MT
+    steps = 2 * tiles
+    wide = gq.shape[1]
+    part = dwo_in.shape[0] // steps
+    outs = (dq_out, dk_out)
+
+    def rows(m, size=MT):
+        return pl.ds(pl.multiple_of(m * size, size), size)
+
+    ht_loads = [pltpu.make_async_copy(ht.at[rows(m), :], ht_v.at[rows(m), :], hsem.at[m]) for m in range(tiles)]
+    g_loads = [pltpu.make_async_copy(x, g2.at[k], gsem.at[k]) for k, x in enumerate((gq, gk))]
+    row_in = [pltpu.make_async_copy(a_in, a_v, rsem.at[0]), pltpu.make_async_copy(dx_in, dx_v, rsem.at[1])]
+    row_out = [pltpu.make_async_copy(a_v, a_out, rsem.at[0]), pltpu.make_async_copy(dx_v, dx_out, rsem.at[1])]
+
+    def bring(k, it):
+        src, buf = ((dwo_in, dwo_v), (dwv_in, dwv_v))[k]
+        return pltpu.make_async_copy(src.at[rows(it, part), :], buf.at[rows(it, part), :], isem.at[k, it])
+
+    def put(k, it):
+        buf, dst = ((dwo_v, dwo_out), (dwv_v, dwv_out))[k]
+        return pltpu.make_async_copy(buf.at[rows(it, part), :], dst.at[rows(it, part), :], osem.at[k, it])
 
     def store(slot, out, m):
         return pltpu.make_async_copy(out_v.at[slot], out.at[rows(m), :], usem.at[slot])
 
-    def product(slot, a, b):
-        for n in range(0, wide, NT):
-            out_v[slot, :, n:n + NT] = nn(a, b[:, n:n + NT]).astype(BF16)
-
-    def turn(m):
-        ht_v[rows(m), :] = h_v[:, rows(m)].T
-
-    for m in range(tiles):
-        ot_loads[m].wait()
-        if m == 0:
-            g_load.wait()
-        if m == 1:
-            h_load.wait()
-        if m >= 2:
-            store(m % 2, do_out, m - 2).wait()
-        if m >= 1:
-            turn(m - 1)
-        product(m % 2, ot_v[m * MT:(m + 1) * MT, :], g_v)
-        store(m % 2, do_out, m).start()
-
-    turn(tiles - 1)
-    for c in small_in:
-        c.wait()
-    for c in small_out:
+    ht_loads[0].start()
+    g_loads[0].start()
+    for c in ht_loads[1:] + g_loads[1:] + row_in:
         c.start()
-
-    @pl.loop(0, 3 * tiles)
+    for it in range(steps):
+        for k in range(2):
+            bring(k, it).start()
+    dl_out[...] = dl_in[...]
+
+    @pl.loop(0, steps)
     def _(it):
         k, m, slot = it // tiles, lax.rem(it, tiles), lax.rem(it, 2)
-        for j in range(3):
+        for j in range(tiles):
+            @pl.when(it == j)
+            def _():
+                ht_loads[j].wait()
+        for j in range(2):
             @pl.when(it == j * tiles)
             def _():
-                g3_loads[j].wait()
-
-        store(slot, do_out, 0).wait()
-        product(slot, ht_v[rows(m), :], g3.at[k])
-        for j in range(3):
+                g_loads[j].wait()
+
+        @pl.when(it == 1)
+        def _():
+            for c, d in zip(row_in, row_out):
+                c.wait()
+                d.start()
+
+        @pl.when(it >= 2)
+        def _():
+            store(slot, dq_out, 0).wait()
+
+        for n in range(0, wide, NT):
+            out_v[slot, :, n:n + NT] = nn(ht_v[rows(m), :], g2[k, :, n:n + NT]).astype(BF16)
+        for j in range(2):
             @pl.when(k == j)
             def _():
                 store(slot, outs[j], m).start()
+            bring(j, it).wait()
+            put(j, it).start()
 
     for slot in range(2):
-        store(slot, do_out, 0).wait()
-    for c in small_out:
-        c.wait()
-
-
-def run_grads(h, g, ot, gq, gk, gv, attn_out, d_hid, d_lnw):
-    seq, model = h.shape
+        store(slot, dq_out, 0).wait()
+    for it in range(steps):
+        for k in range(2):
+            put(k, it).wait()
+    for d in row_out:
+        d.wait()
+
+
+def run_grads(ht, dwo, gq, gk, dwv, attn_out, d_hid, d_lnw):
+    model, seq = ht.shape
     wide = gq.shape[1]
     tiles = model // MT
     hbm = pl.BlockSpec(memory_space=pl.ANY)
     vm = pl.BlockSpec(memory_space=pltpu.VMEM)
-    grad = jax.ShapeDtypeStruct((model, wide), BF16)
 
     def like(a):
         return jax.ShapeDtypeStruct(a.shape, a.dtype)
 
+    grad = jax.ShapeDtypeStruct((model, wide), BF16)
     return pl.pallas_call(
         grad_kernel,
-        out_shape=[grad, grad, grad, jax.ShapeDtypeStruct((wide, model), BF16),
-                   like(attn_out), like(d_hid), like(d_lnw)],
-        in_specs=[hbm] * 8 + [vm],
+        out_shape=[grad, grad, like(dwo), like(dwv), like(attn_out), like(d_hid), like(d_lnw)],
+        in_specs=[hbm] * 7 + [vm],
         out_specs=[hbm] * 6 + [vm],
         scratch_shapes=[
-            pltpu.VMEM((wide, seq), BF16),
-            pltpu.VMEM((seq, model), BF16),
-            pltpu.VMEM((seq, model), BF16),
             pltpu.VMEM((model, seq), BF16),
-            pltpu.VMEM((3, seq, wide), BF16),
+            pltpu.VMEM((2, seq, wide), BF16),
             pltpu.VMEM((2, MT, wide), BF16),
+            pltpu.VMEM(dwo.shape, BF16),
+            pltpu.VMEM(dwv.shape, BF16),
             pltpu.VMEM(attn_out.shape, BF16),
             pltpu.VMEM(d_hid.shape, BF16),
-            pltpu.SemaphoreType.DMA((7,)),
             pltpu.SemaphoreType.DMA((tiles,)),
+            pltpu.SemaphoreType.DMA((2,)),
+            pltpu.SemaphoreType.DMA((2,)),
+            pltpu.SemaphoreType.DMA((2, 2 * tiles)),
+            pltpu.SemaphoreType.DMA((2, 2 * tiles)),
             pltpu.SemaphoreType.DMA((2,)),
         ],
         compiler_params=pltpu.CompilerParams(vmem_limit_bytes=VMEM_LIMIT),
         name="weight_grads",
-    )(ot, g, h, gq, gk, gv, attn_out, d_hid, d_lnw)
+    )(ht, gq, gk, dwo, dwv, attn_out, d_hid, d_lnw)
 
 
 def solution(mesh):
@@ -594,9 +655,8 @@
     grad_spec = P('dp', None)
 
     def local_step(hidden, positions, d_attn, ln_weight, w_q, w_k, w_v, w_o):
-        h, g, ot, gq, gk, gv, attn_out, d_hid, d_lnw = run_main(
-            n_dev, hidden, d_attn, positions, ln_weight, w_q, w_k, w_v, w_o)
-        dwq, dwk, dwv, dwo, attn_out, d_hid, d_lnw = run_grads(h, g, ot, gq, gk, gv, attn_out, d_hid, d_lnw)
+        parts = run_main(n_dev, hidden, d_attn, positions, ln_weight, w_q, w_k, w_v, w_o)
+        dwq, dwk, dwo, dwv, attn_out, d_hid, d_lnw = run_grads(*parts)
         return attn_out, d_hid, d_lnw, dwq, dwk, dwv, dwo
 
     return jax.shard_map(local_step, mesh=mesh,

time: 136 us -> 124 us (0.912)
  Pallas kernels: 134 us -> 122 us
    pallas_call x2, Pallas kernels: 134 us -> 122 us  [the longest x1 92.9 us: run_main(): pl.pallas_call(functools.partial(main_kernel, n_dev), out_shape=(jax.Shap...]
where the time goes in v2:
time: 124 us
  Pallas kernels  122 us (98%)
    pallas_call x1, Pallas kernels, run_main(): pl.pallas_call(functools.partial(main_kernel, n_dev), out_shape=(jax.Shap...  92.9 us
    pallas_call x1, Pallas kernels, run_grads(): pl.pallas_call(grad_kernel, out_shape=[grad, grad, like(dwo), like(dwv),...  29.6 us

profile of v2, /device:TPU:81, one launch (start us, length us, event | category | flops | bytes accessed | tf_op | source)
XLA Modules:
  0.0 124.0 jit_solution(17128870341142617980)
XLA Ops:
  0.6 0.1 broadcast_in_dim.3
  0.7 0.7 broadcast_in_dim_reshape.3.f_ref
  1.4 92.9 %gather_attention.1 = (bf16[2048,1024]{1,0:T(8,128)(2,1)}, bf16[2048,2048]{1,0:T(8,128)(2,1)}, bf16[1024,2048]{1,0:T(8,128)(2,1)}, bf16[1024,2048]{1,0:T(8,128)(...) custom-call(bf16[128,2048]{1,0:T(8,128)(2,1)} %x_ref.1, ...), custom_call_target="tpu_custom_call" | custom-call | tf_op jit(solution)/shard_map/gather_attention/pallas_call | solution.py:491
  94.3 29.6 %weight_grads.1 = (bf16[2048,2048]{1,0:T(8,128)(2,1)}, bf16[2048,2048]{1,0:T(8,128)(2,1)}, bf16[2048,2048]{1,0:T(8,128)(2,1)}, bf16[2048,2048]{1,0:T(8,128)(2,1)...) custom-call(bf16[2048,1024]{1,0:T(8,128)(2,1)} %get-tuple-element.22.ht, ...), custom_call_target="tpu_custom_call" | custom-call | tf_op jit(solution)/shard_map/weight_grads/pallas_call | solution.py:626
  (1 shorter events, 0.0 us)

commit v3 on v2

--- a/solution.py
+++ b/solution.py
@@ -2,6 +2,7 @@
 
 import jax
 import jax.numpy as jnp
+import numpy as np
 from jax import lax
 from jax.experimental import pallas as pl
 from jax.experimental.pallas import tpu as pltpu
@@ -283,8 +284,8 @@
     def head_cols(n):
         return pl.ds(pl.multiple_of(my_col + n * HEAD_DIM, HEAD_DIM), HEAD_DIM)
 
-    def rows_tile(m):
-        return pl.ds(pl.multiple_of(m * MT, MT), MT)
+    def rows_tile(m, size=QB):
+        return pl.ds(pl.multiple_of(m * size, size), size)
 
     def in_turn(streams):
         while streams:
@@ -363,14 +364,6 @@
     ht_copy = pltpu.make_async_copy(wot_s, ht_out, lsem.at[0])
     ht_copy.start()
 
-    @pl.loop(0, width // MT)
-    def _(m):
-        per = MT // HEAD_DIM
-        o_t = jnp.concatenate([ot_s[m * per + n] for n in range(per)], axis=0)
-        for n in range(0, model, NT):
-            h_all[rows_tile(m), n:n + NT] = nn(o_t, g_all[:, n:n + NT]).astype(BF16)
-        give(0, h_all.at[rows_tile(m), :], dwo_out.at[pl.ds(pl.multiple_of(my_col + m * MT, MT), MT), :])
-
     def at(j, i):
         return i * (i + 1) // 2 + j
 
@@ -379,21 +372,15 @@
         kt[...] = qkv[1, n].T
         for i in reversed(range(nq)):
             q_i, do_i = qkv[0, n, tile(i), :], do_s[n, tile(i), :]
+            ss = [scores(n, i, j) for j in range(i + 1)]
+            dps = [nt(qkv[2, n, tile(j), :], do_i) for j in range(i + 1)]
+            yield True
             m, li = m_s[n, :, tile(i)], li_s[n, :, tile(i)]
-            ps, ts, rdot = [], [], 0.0
-            s, dp = scores(n, i, 0), nt(qkv[2, n, tile(0), :], do_i)
+            ps = [jnp.exp2((s - m) * c2) * li for s in ss]
+            ts = [p * dp for p, dp in zip(ps, dps)]
+            rdot = sum(jnp.sum(t, axis=0, keepdims=True) for t in ts)
             for j in range(i + 1):
-                yield True
-                p = jnp.exp2((s - m) * c2) * li
-                t = p * dp
-                rdot = rdot + jnp.sum(t, axis=0, keepdims=True)
-                pt[at(j, i)] = p.astype(BF16)
-                ps.append(p)
-                ts.append(t)
-                if j < i:
-                    s, dp = scores(n, i, j + 1), nt(qkv[2, n, tile(j + 1), :], do_i)
-            yield True
-            for j in range(i + 1):
+                pt[at(j, i)] = ps[j].astype(BF16)
                 dst[at(j, i)] = ((ts[j] - ps[j] * rdot) * SCALE).astype(BF16)
             yield True
             dq = sum(nn(kt[:, tile(j)], dst[at(j, i)]) for j in range(i + 1)).T.astype(BF16).astype(F32)
@@ -404,9 +391,16 @@
             res[2, n, tile(i), :] = sum(nn(pt[at(i, k)], do_s[n, tile(k), :]) for k in range(i, nq)).astype(BF16)
             yield True
 
+    def out_grad(t):
+        o_t = jnp.concatenate([ot_s[2 * t], ot_s[2 * t + 1]], axis=0)
+        for n in range(0, model, QB):
+            h_all[rows_tile(t), n:n + QB] = nn(o_t, g_all[:, n:n + QB]).astype(BF16)
+            yield True
+
     @pl.loop(0, heads // 2)
     def _(t):
-        in_turn([backward(2 * t, 0), backward(2 * t + 1, 1)])
+        in_turn([backward(2 * t, 0), backward(2 * t + 1, 1), out_grad(t)])
+        give(0, h_all.at[rows_tile(t), :], dwo_out.at[pl.ds(pl.multiple_of(my_col + t * QB, QB), QB), :])
         for a in (1, 2):
             for n in (2 * t, 2 * t + 1):
                 give(a, res.at[a - 1, n], outs[a].at[:, head_cols(n)])
@@ -449,11 +443,11 @@
         place = pl.ds(pl.multiple_of(lax.rem(m, per) * MT, MT), MT)
         for part in range(0, heads, 4):
             gv = jnp.concatenate([res[2, part + n] for n in range(4)], axis=1)
-            y = nn(wot_s[rows_tile(m), :], gv).astype(BF16)
+            y = nn(wot_s[rows_tile(m, MT), :], gv).astype(BF16)
             for n in range(4):
                 qkv[m // per, part + n, place, :] = y[:, n * HEAD_DIM:(n + 1) * HEAD_DIM]
         for n in range(heads):
-            give(3, qkv.at[m // per, n, place, :], dwv_out.at[rows_tile(m), head_cols(n)])
+            give(3, qkv.at[m // per, n, place, :], dwv_out.at[rows_tile(m, MT), head_cols(n)])
 
     ht_copy.wait()
     for kind, (block, piece, to) in sends.items():
@@ -487,7 +481,7 @@
     full = w_q.shape[1]
     wide = jax.ShapeDtypeStruct((seq, full), BF16)
     rows = jax.ShapeDtypeStruct((blk, model), BF16)
-    freq = jnp.repeat(ROPE_BASE ** (-jnp.arange(0, HEAD_DIM, 2, dtype=F32) / HEAD_DIM), 2)[None, :]
+    freq = np.repeat(ROPE_BASE ** (-np.arange(0, HEAD_DIM, 2) / HEAD_DIM), 2)[None, :].astype(np.float32)
     return pl.pallas_call(
         functools.partial(main_kernel, n_dev),
         out_shape=(jax.ShapeDtypeStruct((model, seq), BF16), jax.ShapeDtypeStruct((full, model), BF16),
@@ -567,9 +561,8 @@
     g_loads[0].start()
     for c in ht_loads[1:] + g_loads[1:] + row_in:
         c.start()
-    for it in range(steps):
-        for k in range(2):
-            bring(k, it).start()
+    for k in range(2):
+        bring(k, 0).start()
     dl_out[...] = dl_in[...]
 
     @pl.loop(0, steps)
@@ -602,6 +595,10 @@
                 store(slot, outs[j], m).start()
             bring(j, it).wait()
             put(j, it).start()
+
+            @pl.when(it < steps - 1)
+            def _():
+                bring(j, it + 1).start()
 
     for slot in range(2):
         store(slot, dq_out, 0).wait()

time: 124 us -> 120 us (0.968)
  Pallas kernels: 122 us -> 119 us
    pallas_call x1, Pallas kernels: 29.6 us -> 27.7 us  [run_grads(): pl.pallas_call(grad_kernel, out_shape=[grad, grad, like(dwo), like(dwv),...]
    pallas_call x1, Pallas kernels: 92.9 us -> 91.2 us  [run_main(): pl.pallas_call(functools.partial(main_kernel, n_dev), out_shape=(jax.Shap...]
where the time goes in v3:
time: 120 us
  Pallas kernels  119 us (99%)
    pallas_call x1, Pallas kernels, run_main(): pl.pallas_call(functools.partial(main_kernel, n_dev), out_shape=(jax.Shap...  91.2 us
    pallas_call x1, Pallas kernels, run_grads(): pl.pallas_call(grad_kernel, out_shape=[grad, grad, like(dwo), like(dwv),...  27.7 us

profile of v3, /device:TPU:81, one launch (start us, length us, event | category | flops | bytes accessed | tf_op | source)
XLA Modules:
  0.0 119.6 jit_solution(2499892955780092863)
XLA Ops:
  0.6 91.2 %gather_attention.1 = (bf16[2048,1024]{1,0:T(8,128)(2,1)}, bf16[2048,2048]{1,0:T(8,128)(2,1)}, bf16[1024,2048]{1,0:T(8,128)(2,1)}, bf16[1024,2048]{1,0:T(8,128)(...) custom-call(bf16[128,2048]{1,0:T(8,128)(2,1)} %x_ref.1, ...), custom_call_target="tpu_custom_call" | custom-call | tf_op jit(solution)/shard_map/gather_attention/pallas_call | solution.py:485
  91.8 27.7 %weight_grads.1 = (bf16[2048,2048]{1,0:T(8,128)(2,1)}, bf16[2048,2048]{1,0:T(8,128)(2,1)}, bf16[2048,2048]{1,0:T(8,128)(2,1)}, bf16[2048,2048]{1,0:T(8,128)(2,1)...) custom-call(bf16[2048,1024]{1,0:T(8,128)(2,1)} %get-tuple-element.22.ht, ...), custom_call_target="tpu_custom_call" | custom-call | tf_op jit(solution)/shard_map/weight_grads/pallas_call | solution.py:623

commit v4 on v3

--- a/solution.py
+++ b/solution.py
@@ -307,16 +307,19 @@
     def forward(n, slot):
         vt = vt_s.at[slot]
         vt[...] = qkv[2, n].T
+        ss = [scores(n, 0, 0)]
+        yield True
         for i in range(nq):
-            ss = [scores(n, i, j) for j in range(i + 1)]
+            now = ss
+            if i + 1 < nq:
+                ss = [scores(n, i + 1, j) for j in range(i + 2)]
             yield True
-            m = functools.reduce(jnp.maximum, [jnp.max(s, axis=0, keepdims=True) for s in ss])
-            es = [jnp.exp2((s - m) * c2) for s in ss]
-            li = 1.0 / sum(jnp.sum(e, axis=0, keepdims=True) for e in es)
+            m = jnp.max(functools.reduce(jnp.maximum, now), axis=0, keepdims=True)
+            es = [jnp.exp2((s - m) * c2) for s in now]
+            li = 1.0 / jnp.sum(sum(es), axis=0, keepdims=True)
             m_s[n, :, tile(i)] = m
             li_s[n, :, tile(i)] = li
             ps = [(e * li).astype(BF16) for e in es]
-            yield True
             ot_s[n, :, tile(i)] = sum(nn(vt[:, tile(j)], p) for j, p in enumerate(ps)).astype(BF16)
             yield True
 
@@ -326,7 +329,9 @@
         def _():
             pass_first(1)
 
-        in_turn([forward(2 * t, 0), forward(2 * t + 1, 1)])
+        first = forward(2 * t, 0)
+        next(first)
+        in_turn([first, forward(2 * t + 1, 1)])
 
     here = pl.ds(pl.multiple_of(chip * rows_chip, rows_chip), rows_chip)
     mine = pl.ds(pl.multiple_of(core * blk, blk), blk)
@@ -370,18 +375,25 @@
     def backward(n, slot):
         kt, pt, dst = kt_s.at[slot], pt_s.at[slot], dst_s.at[slot]
         kt[...] = qkv[1, n].T
+        def products(i):
+            q_i, do_i = qkv[0, n, tile(i), :], do_s[n, tile(i), :]
+            return ([scores(n, i, j) for j in range(i + 1)],
+                    [nt(qkv[2, n, tile(j), :], do_i) for j in range(i + 1)])
+
+        ahead = products(nq - 1)
+        yield True
         for i in reversed(range(nq)):
-            q_i, do_i = qkv[0, n, tile(i), :], do_s[n, tile(i), :]
-            ss = [scores(n, i, j) for j in range(i + 1)]
-            dps = [nt(qkv[2, n, tile(j), :], do_i) for j in range(i + 1)]
-            yield True
+            ss, dps = ahead
             m, li = m_s[n, :, tile(i)], li_s[n, :, tile(i)]
             ps = [jnp.exp2((s - m) * c2) * li for s in ss]
             ts = [p * dp for p, dp in zip(ps, dps)]
-            rdot = sum(jnp.sum(t, axis=0, keepdims=True) for t in ts)
+            rdot = jnp.sum(sum(ts), axis=0, keepdims=True)
             for j in range(i + 1):
                 pt[at(j, i)] = ps[j].astype(BF16)
                 dst[at(j, i)] = ((ts[j] - ps[j] * rdot) * SCALE).astype(BF16)
+            yield True
+            if i:
+                ahead = products(i - 1)
             yield True
             dq = sum(nn(kt[:, tile(j)], dst[at(j, i)]) for j in range(i + 1)).T.astype(BF16).astype(F32)
             c, s = cos_s[tile(i), :], sin_s[tile(i), :]

time: 120 us -> 118 us (0.983)
  Pallas kernels: 119 us -> 116 us
    pallas_call x1, Pallas kernels: 91.2 us -> 88.7 us  [run_main(): pl.pallas_call(functools.partial(main_kernel, n_dev), out_shape=(jax.Shap...]
where the time goes in v4:
time: 118 us; the launch traced here: 117 us
  Pallas kernels  116 us (98%)
    pallas_call x1, Pallas kernels, run_main(): pl.pallas_call(functools.partial(main_kernel, n_dev), out_shape=(jax.Shap...  88.7 us
    pallas_call x1, Pallas kernels, run_grads(): pl.pallas_call(grad_kernel, out_shape=[grad, grad, like(dwo), like(dwv),...  27.7 us

profile of v4, /device:TPU:81, one launch (start us, length us, event | category | flops | bytes accessed | tf_op | source)
XLA Modules:
  0.0 117.2 jit_solution(12330669740423317099)
XLA Ops:
  0.6 88.7 %gather_attention.1 = (bf16[2048,1024]{1,0:T(8,128)(2,1)}, bf16[2048,2048]{1,0:T(8,128)(2,1)}, bf16[1024,2048]{1,0:T(8,128)(2,1)}, bf16[1024,2048]{1,0:T(8,128)(...) custom-call(bf16[128,2048]{1,0:T(8,128)(2,1)} %x_ref.1, ...), custom_call_target="tpu_custom_call" | custom-call | tf_op jit(solution)/shard_map/gather_attention/pallas_call | solution.py:497
  89.4 27.7 %weight_grads.1 = (bf16[2048,2048]{1,0:T(8,128)(2,1)}, bf16[2048,2048]{1,0:T(8,128)(2,1)}, bf16[2048,2048]{1,0:T(8,128)(2,1)}, bf16[2048,2048]{1,0:T(8,128)(2,1)...) custom-call(bf16[2048,1024]{1,0:T(8,128)(2,1)} %get-tuple-element.22.ht, ...), custom_call_target="tpu_custom_call" | custom-call | tf_op jit(solution)/shard_map/weight_grads/pallas_call | solution.py:635
